TPU v7x, 256 devices: a whole 4x4x8 slice. The times are simulated.
256 devices in a mesh: sx: 8 (over y, core), sy: 8 (over z), af: 4 (over x).
Axes of the slice: x: 4, y: 4, z: 8, core: 2. Of those that a mesh axis runs over, the one named last changes fastest.
Arguments:
- sky_maps: float32 [256, 256, 1024], P('sx', 'sy', 'af'), may hold values from -16 to 25
- validity: int32 [256, 256], P('sx', 'sy'), may hold values 0 or 1
- row_taps: float32 [1024, 65], P('af'), may hold values from -0.75 to 0.75
- column_taps: float32 [1024, 65], P('af'), may hold values from -0.75 to 0.75
- init_loadings: float32 [1024, 32], P('af'), may hold values from -0.1875 to 0.1875
Outputs:
- cleaned_maps: float32 [256, 256, 1024], P('sx', 'sy', 'af')
- loadings: float32 [1024, 32], P('af')
- noise_var: float32 [], replicated
All inputs are finite; a program needn't handle non-finite values. No bound on the sum of `validity` on one device may be relied on, other than what follows from the above.
Results may differ from a plain program's by a relative error of at most 0.0003.
Values sent between devices are 32-bit elements; how exact they have to be, the bound alone decides.
No kernel may reach another device: no remote copies, remote signals or barrier semaphores. Data moves between devices by JAX's collectives and lax.ppermute only.
A program may use at most 128 MiB of HBM per device.

v0:
```python
import math
import jax
import jax.numpy as jnp
from jax import lax
from jax.sharding import PartitionSpec as P

ITERS = 4
HIGHEST_PRECISION = lax.Precision.HIGHEST


def padded(block, sides, width):
    for axis, dim in sides:
        count = lax.axis_size(axis)
        forward = [(i, i + 1) for i in range(count - 1)]
        backward = [(target, source) for source, target in forward]
        low = lax.ppermute(
            lax.slice_in_dim(block, block.shape[dim] - width, None, axis=dim), axis, forward
        )
        high = lax.ppermute(lax.slice_in_dim(block, 0, width, axis=dim), axis, backward)
        block = jnp.concatenate([low, block, high], axis=dim)
    return block


def inverse_spd(matrix):
    identity = jnp.eye(matrix.shape[0], dtype=matrix.dtype)
    factor = jnp.linalg.cholesky(matrix)
    lower_inverse = lax.linalg.triangular_solve(factor, identity, left_side=True, lower=True)
    return jnp.dot(lower_inverse.T, lower_inverse, precision=HIGHEST_PRECISION)


def contract_rows(left_rows, right_rows):
    return lax.dot_general(
        left_rows, right_rows, (((0,), (0,)), ((), ())), precision=HIGHEST_PRECISION
    )


def correlate(extended, tap_table, out_length, along_dim):
    freq_count, tap_count = tap_table.shape
    block_size = math.gcd(freq_count, 32)
    in_length = extended.shape[along_dim]
    offsets = jnp.arange(in_length)[:, None] - jnp.arange(out_length)[None, :]
    one_hot = (offsets[None, :, :] == jnp.arange(tap_count)[:, None, None]).astype(jnp.float32)
    shape_out = list(extended.shape)
    shape_out[along_dim] = out_length
    filtered_all = jnp.zeros(tuple(shape_out), jnp.float32)

    def add_block(block_index, filtered_all):
        first_freq = block_index * block_size
        slab_part = lax.dynamic_slice_in_dim(extended, first_freq, block_size, 2)
        tap_block = lax.dynamic_slice_in_dim(tap_table, first_freq, block_size, 0)
        band_matrix = jnp.einsum("ft,tio->fio", tap_block, one_hot, precision=HIGHEST_PRECISION)
        if along_dim == 0:
            filtered = jnp.einsum(
                "icf,fio->ocf", slab_part, band_matrix, precision=HIGHEST_PRECISION
            )
        else:
            filtered = jnp.einsum(
                "rif,fio->rof", slab_part, band_matrix, precision=HIGHEST_PRECISION
            )
        return lax.dynamic_update_slice_in_dim(filtered_all, filtered, first_freq, 2)

    return lax.fori_loop(0, freq_count // block_size, add_block, filtered_all)


def body(sky_maps, validity, row_taps, column_taps, init_loadings):
    rows_here, cols_here, freqs_here = sky_maps.shape
    halo_width = (row_taps.shape[1] - 1) // 2
    masked = sky_maps * validity.astype(jnp.float32)[:, :, None]
    extended = padded(masked, (("sx", 0), ("sy", 1)), halo_width)
    smoothed = correlate(extended, row_taps, rows_here, 0)
    beamed = correlate(smoothed, column_taps, cols_here, 1)
    spectra = beamed.reshape(rows_here * cols_here, freqs_here)
    total_power = lax.psum(jnp.sum(spectra * spectra), ("sx", "sy", "af"))
    pixel_count = rows_here * cols_here * lax.axis_size("sx") * lax.axis_size("sy")
    freq_total = freqs_here * lax.axis_size("af")
    components = init_loadings.shape[1]
    identity = jnp.eye(components, dtype=jnp.float32)
    noise_var = jnp.float32(1.0)
    loadings = lax.all_gather(init_loadings, "af", axis=0, tiled=True)
    pixel_rows = lax.all_to_all(spectra, "af", split_axis=0, concat_axis=1, tiled=True)
    for iteration in range(ITERS):
        inverse = inverse_spd(contract_rows(loadings, loadings) + noise_var * identity)
        latent = jnp.dot(
            pixel_rows,
            jnp.dot(loadings, inverse, precision=HIGHEST_PRECISION),
            precision=HIGHEST_PRECISION,
        )
        cross_moment, second = lax.psum(
            (contract_rows(pixel_rows, latent), contract_rows(latent, latent)), ("sx", "sy", "af")
        )
        scaled = pixel_count * noise_var * inverse + second
        updated = jnp.dot(cross_moment, inverse_spd(scaled), precision=HIGHEST_PRECISION)
        new_gram = contract_rows(updated, updated)
        noise_var = (
            total_power - 2.0 * jnp.sum(updated * cross_moment) + jnp.sum(scaled * new_gram)
        ) / (pixel_count * freq_total)
        loadings = updated
    inverse = inverse_spd(contract_rows(loadings, loadings) + noise_var * identity)
    latent = jnp.dot(
        pixel_rows,
        jnp.dot(loadings, inverse, precision=HIGHEST_PRECISION),
        precision=HIGHEST_PRECISION,
    )
    cleaned_rows = pixel_rows - jnp.dot(latent, loadings.T, precision=HIGHEST_PRECISION)
    cleaned = lax.all_to_all(cleaned_rows, "af", split_axis=1, concat_axis=0, tiled=True)
    loadings_block = lax.dynamic_slice_in_dim(
        loadings, lax.axis_index("af") * freqs_here, freqs_here, 0
    )
    return (cleaned.reshape(rows_here, cols_here, freqs_here), loadings_block, noise_var)


def solution(mesh):
    placed = (P("sx", "sy", "af"), P("sx", "sy"), P("af", None), P("af", None), P("af", None))
    return jax.shard_map(
        body,
        mesh=mesh,
        in_specs=placed,
        out_specs=(P("sx", "sy", "af"), P("af", None), P()),
        check_vma=False,
    )
```

profile of v0, /device:TPU:32, one launch (start us, length us, event | category | flops | bytes accessed | tf_op | source)
XLA Modules:
  0.0 1608.8 jit_solution(8080160736587513446)
XLA Ops:
  13.4 3.6 collective-permute-done.1
  17.0 2.0 pad_maximum_fusion.1
  19.1 3.8 collective-permute-start.2
  22.9 3.7 collective-permute-start.3
  26.8 12.6 all_gather.3
  41.6 3.6 cholesky.149
  47.2 3.8 custom-call.13
  51.0 29.7 %collective-permute-done.2 = f32[96,32,256]{2,1,0:T(8,128)} collective-permute-done((f32[96,32,256]{2,1,0:T(8,128)}, f32[96,32,256]{2,1,0:T(8,128)}, u32[]{:S(2)}, u32[]{:S(2)}) %collective-permute-start.2) | collective-permute-done | bytes 3145760 | tf_op jit(solution)/shard_map/ppermute | solution.py:16
  80.7 3.9 collective-permute-done.3
  84.7 5.9 pad_maximum_fusion
  90.6 11.6 copy.69
  102.2 2.5 broadcast_in_dim.5
  104.7 38.0 %while.28 = (s32[]{:T(128)}, f32[32,96,256]{1,0,2:T(8,128)}, f32[256,65]{1,0:T(8,128)S(1)}, f32[96,96,256]{1,0,2:T(8,128)}, s32[96,32]{0,1:T(8,128)S(1)}, /*index=5*/s32[]{:T(128)}, s32[]{:T(128)}, s32[]{:T(128)}, s32[]{:T(128)}) while((s32[]{:T(128)}, f32[32,96,256]{1,0,2:T(8,128)}, f32[256,65]{1,0:T(8,128)S(1)}, ...), condition=%wide.region_1.0_spmd.clone, body=%wide.region_0.0_spmd.clone.sunk | while | flops 190322688 | bytes 2917519 | solution.py:62
  105.5 4.0 fusion.193
  110.2 4.0 fusion.193
  115.0 3.9 fusion.193
  119.7 3.9 fusion.193
  124.5 3.9 fusion.193
  129.2 3.9 fusion.193
  134.0 3.9 fusion.193
  138.7 3.9 fusion.193
  142.6 2.5 broadcast_in_dim.4
  145.1 31.1 %while.29 = (s32[]{:T(128)}, f32[32,32,256]{0,1,2:T(8,128)}, f32[256,65]{1,0:T(8,128)S(1)}, f32[32,96,256]{1,0,2:T(8,128)}, s32[96,32]{0,1:T(8,128)S(1)}, /*index=5*/s32[]{:T(128)}, s32[]{:T(128)}, s32[]{:T(128)}, s32[]{:T(128)}) while((s32[]{:T(128)}, f32[32,32,256]{0,1,2:T(8,128)}, f32[256,65]{1,0:T(8,128)S(1)}, ...), condition=%wide.region_3.0_spmd.clone, body=%wide.region_2.0_spmd.clone.sunk | while | flops 114825224 | bytes 1868943 | solution.py:62
  145.9 3.1 fusion.199
  149.8 3.1 fusion.199
  153.6 3.1 fusion.199
  157.5 3.1 fusion.199
  161.4 3.1 fusion.199
  165.3 3.1 fusion.199
  169.2 3.1 fusion.199
  173.1 3.1 fusion.199
  176.2 4.7 copy.71
  180.9 4.3 all-to-all-start
  186.0 3.9 multiply_reduce_fusion
  189.9 6.2 all-to-all-done
  198.8 102.3 %all-reduce = (f32[32,32]{0,1:T(8,128)S(1)}, f32[]{:T(128)}) all-reduce(f32[32,32]{0,1:T(8,128)S(1)} %fusion.79, f32[]{:T(128)} %multiply_reduce_fusion), channel_id=1, replica_groups=mesh['sx'=8,'sy'=8,'af'=4] {'sx','sy','af'}, use_global_device_ids=true, to_apply=%region_7.10 | all-reduce | flops 1025 | bytes 8200 | tf_op jit(solution)/shard_map/psum | solution.py:88
  301.1 2.9 cholesky.160
  305.4 2.4 custom-call.14
  308.4 241.5 %all-reduce.6.cloned.1.call-done = f32[1024,32]{0,1:T(8,128)} async-done(((f32[1024,32]{0,1:T(8,128)}), f32[1024,32]{0,1:T(8,128)}) %all-reduce.6.cloned.1.call-update) | async-done | bytes 131088 | tf_op jit(solution)/shard_map/psum | solution.py:88
  554.7 2.9 cholesky.171
  558.9 2.4 custom-call.15
  564.8 75.9 %psum.67 = f32[32,32]{0,1:T(8,128)S(1)} all-reduce(f32[32,32]{0,1:T(8,128)S(1)} %fusion.85), channel_id=1, replica_groups=mesh['sx'=8,'sy'=8,'af'=4] {'sx','sy','af'}, use_global_device_ids=true, to_apply=%region_13.16 | all-reduce | flops 1024 | bytes 8192 | tf_op jit(solution)/shard_map/psum | solution.py:88
  640.7 2.9 cholesky.182
  645.0 2.4 custom-call.16
  648.0 240.3 %all-reduce.8.cloned.1.call-done = f32[1024,32]{0,1:T(8,128)} async-done(((f32[1024,32]{0,1:T(8,128)}), f32[1024,32]{0,1:T(8,128)}) %all-reduce.8.cloned.1.call-update) | async-done | bytes 131088 | tf_op jit(solution)/shard_map/psum | solution.py:88
  888.2 1.9 multiply_reduce_fusion.3
  893.1 2.9 cholesky.193
  897.3 2.4 custom-call.17
  903.2 75.9 %psum.69 = f32[32,32]{0,1:T(8,128)S(1)} all-reduce(f32[32,32]{0,1:T(8,128)S(1)} %fusion.91), channel_id=1, replica_groups=mesh['sx'=8,'sy'=8,'af'=4] {'sx','sy','af'}, use_global_device_ids=true, to_apply=%region_17.20 | all-reduce | flops 1024 | bytes 8192 | tf_op jit(solution)/shard_map/psum | solution.py:88
  979.1 2.9 cholesky.204
  983.4 2.4 custom-call.18
  986.6 240.1 %all-reduce.10.cloned.1.call-done = f32[1024,32]{0,1:T(8,128)} async-done(((f32[1024,32]{0,1:T(8,128)}), f32[1024,32]{0,1:T(8,128)}) %all-reduce.10.cloned.1.call-update) | async-done | bytes 131088 | tf_op jit(solution)/shard_map/psum | solution.py:88
  1226.7 1.9 multiply_reduce_fusion.2
  1231.5 2.9 cholesky.215
  1235.8 2.4 custom-call.19
  1241.6 75.9 %psum.71 = f32[32,32]{0,1:T(8,128)S(1)} all-reduce(f32[32,32]{0,1:T(8,128)S(1)} %fusion.97), channel_id=1, replica_groups=mesh['sx'=8,'sy'=8,'af'=4] {'sx','sy','af'}, use_global_device_ids=true, to_apply=%region_21.24 | all-reduce | flops 1024 | bytes 8192 | tf_op jit(solution)/shard_map/psum | solution.py:88
  1317.6 2.9 cholesky.226
  1321.8 2.4 custom-call.20
  1324.8 240.3 %all-reduce.12.cloned.1.call-done = f32[1024,32]{0,1:T(8,128)} async-done(((f32[1024,32]{0,1:T(8,128)}), f32[1024,32]{0,1:T(8,128)}) %all-reduce.12.cloned.1.call-update) | async-done | bytes 131088 | tf_op jit(solution)/shard_map/psum | solution.py:88
  1565.1 1.9 multiply_reduce_fusion.1
  1569.9 2.9 cholesky.237
  1574.2 2.4 custom-call.21
  1580.5 4.0 all-to-all-start.1
  1585.1 15.1 all-to-all-done.1
  (142 shorter events, 61.3 us)
Async XLA Ops:
  7.9 18.7 %copy-start = (f32[256,65]{0,1:T(8,128)S(1)}, f32[256,65]{0,1:T(8,128)}, u32[]{:S(2)}) copy-start(f32[256,65]{0,1:T(8,128)} %param.14) | copy-start | bytes 199684
  7.9 18.8 %copy-start.1 = (f32[256,65]{0,1:T(8,128)S(1)}, f32[256,65]{0,1:T(8,128)}, u32[]{:S(2)}) copy-start(f32[256,65]{0,1:T(8,128)} %param.15) | copy-start | bytes 199684
  9.4 4.0 collective-permute-start
  11.2 5.9 collective-permute-start.1
  19.1 61.7 %collective-permute-start.2 = (f32[96,32,256]{2,1,0:T(8,128)}, f32[96,32,256]{2,1,0:T(8,128)}, u32[]{:S(2)}, u32[]{:S(2)}) collective-permute-start(f32[96,32,256]{2,1,0:T(8,128)} %pad_maximum_fusion.1), channel_id=1, source_target_pairs={{0,4},{4,8},{8,12},{12,16},{16,20},{20,24},{24,28},{1,5},{5,9},{9,... | collective-permute-start | bytes 9437192 | tf_op jit(solution)/shard_map/ppermute | solution.py:16
  22.9 61.8 %collective-permute-start.3 = (f32[96,32,256]{2,1,0:T(8,128)}, f32[96,32,256]{2,1,0:T(8,128)}, u32[]{:S(2)}, u32[]{:S(2)}) collective-permute-start(f32[96,32,256]{2,1,0:T(8,128)} %pad_maximum_fusion.1), channel_id=1, source_target_pairs={{4,0},{8,4},{12,8},{16,12},{20,16},{24,20},{28,24},{5,1},{9,5},{13... | collective-permute-start | bytes 9437192 | tf_op jit(solution)/shard_map/ppermute | solution.py:19
  176.2 9.0 copy-start.2
  180.9 15.2 all-to-all-start
  185.2 364.7 %all-reduce.6.cloned.1.call-start = ((), (), s32[]{:S(2)}) async-start(), calls=%async_computation.2 | async-start | bytes 262144 | tf_op jit(solution)/shard_map/psum | solution.py:88
  308.1 580.1 %all-reduce.8.cloned.1.call-start = ((), (), s32[]{:S(2)}) async-start(), calls=%async_computation.3 | async-start | bytes 262144 | tf_op jit(solution)/shard_map/psum | solution.py:88
  647.7 579.0 %all-reduce.10.cloned.1.call-start = ((), (), s32[]{:S(2)}) async-start(), calls=%async_computation.4 | async-start | bytes 262144 | tf_op jit(solution)/shard_map/psum | solution.py:88
  986.1 579.0 %all-reduce.12.cloned.1.call-start = ((), (), s32[]{:S(2)}) async-start(), calls=%async_computation.5 | async-start | bytes 262144 | tf_op jit(solution)/shard_map/psum | solution.py:88
  1580.5 19.7 %all-to-all-start.1 = ((f32[256,4,256]{2,0,1:T(8,128)}), f32[256,4,256]{2,0,1:T(8,128)S(1)}, u32[]{:S(2)}, u32[]{:S(2)}) async-start(f32[256,4,256]{2,0,1:T(8,128)} %bitcast.179), calls=%async_computation.1 | async-start | bytes 2097152 | tf_op jit(solution)/shard_map/all_to_all | solution.py:105
Sparse Core Ops, SparseCore 0:
  308.2 241.6 all-reduce.5
  647.8 240.3 all-reduce.7
  986.2 240.4 all-reduce.9
  1324.7 240.3 all-reduce.11
where the time goes:
time: 1610 us
  waiting for transfers between devices  1020 us (63%)
  blocking collectives  342 us (21%)
  matrix products  98 us (6%)
  other arithmetic  78.2 us (5%)
  local copies, waits for them, and re-layouts  25.8 us (2%)
  between operations  23.1 us (1%)
  starting transfers between devices  19.2 us (1%)
    psum x4, waiting for transfers between devices, body(): lax.psum((contract_rows(pixel_rows, latent), contract_rows(latent, latent...  962 us
    psum x4, blocking collectives, body(): lax.psum((contract_rows(pixel_rows, latent), contract_rows(latent, latent...  330 us
    another operation x27, other arithmetic, inverse_spd(): factor = jnp.linalg.cholesky(matrix)  33.1 us
  transfers between devices with their start and end apart: 10, of which 10 were waited for; matrix products, arithmetic and copies ran while one was open for 1% of the time, Pallas kernels for 0%

commit v1 on v0

--- a/solution.py
+++ b/solution.py
@@ -86,7 +86,8 @@
             precision=HIGHEST_PRECISION,
         )
         cross_moment, second = lax.psum(
-            (contract_rows(pixel_rows, latent), contract_rows(latent, latent)), ("sx", "sy", "af")
+            lax.psum((contract_rows(pixel_rows, latent), contract_rows(latent, latent)), "sx"),
+            ("sy", "af"),
         )
         scaled = pixel_count * noise_var * inverse + second
         updated = jnp.dot(cross_moment, inverse_spd(scaled), precision=HIGHEST_PRECISION)

time: 1610 us -> 1880 us (1.17)
  blocking collectives: 342 us -> 748 us
  waiting for transfers between devices: 1020 us -> 888 us
    psum x4, waiting for transfers between devices: 962 us -> 262 us  [body(): lax.psum((contract_rows(pixel_rows, latent), contract_rows(latent, latent...]
    psum x0 -> x5, blocking collectives: none -> 641 us  [the longest x4 540 us: body(): lax.psum(lax.psum((contract_rows(pixel_rows, latent), contract_rows(laten...]
    psum x0 -> x4, waiting for transfers between devices: none -> 577 us  [body(): lax.psum(lax.psum((contract_rows(pixel_rows, latent), contract_rows(laten...]
    psum x4, blocking collectives: 330 us -> 94.2 us  [body(): lax.psum((contract_rows(pixel_rows, latent), contract_rows(latent, latent...]
  transfers between devices with their start and end apart: 10 -> 14, of which waited for: 10 -> 13; matrix products, arithmetic and copies ran while one was open for 1% -> 1% of each run, Pallas kernels for 0% -> 0%
where the time goes in v1:
time: 1880 us
  waiting for transfers between devices  888 us (47%)
  blocking collectives  748 us (40%)
  matrix products  97.8 us (5%)
  other arithmetic  78.2 us (4%)
  local copies, waits for them, and re-layouts  25.8 us (1%)
  between operations  23.4 us (1%)
  starting transfers between devices  19.6 us (1%)
    psum x4, waiting for transfers between devices, body(): lax.psum(lax.psum((contract_rows(pixel_rows, latent), contract_rows(laten...  577 us
    psum x4, blocking collectives, body(): lax.psum(lax.psum((contract_rows(pixel_rows, latent), contract_rows(laten...  540 us
    psum x4, waiting for transfers between devices, body(): lax.psum((contract_rows(pixel_rows, latent), contract_rows(latent, latent...  262 us
    psum x1, blocking collectives, body(): total_power = lax.psum(jnp.sum(spectra * spectra), ('sx', 'sy', 'af'))  101 us
    psum x4, blocking collectives, body(): lax.psum((contract_rows(pixel_rows, latent), contract_rows(latent, latent...  94.2 us
  transfers between devices with their start and end apart: 14, of which 13 were waited for; matrix products, arithmetic and copies ran while one was open for 1% of the time, Pallas kernels for 0%

profile of v1, /device:TPU:32, one launch (start us, length us, event | category | flops | bytes accessed | tf_op | source)
XLA Modules:
  0.0 1880.7 jit_solution(13578796029791170810)
XLA Ops:
  13.4 3.6 collective-permute-done.1
  19.1 3.8 collective-permute-start.2
  22.9 3.7 collective-permute-start.3
  26.8 12.6 all_gather.3
  41.6 3.6 cholesky.149
  47.2 3.8 custom-call.13
  51.0 29.7 %collective-permute-done.2 = f32[96,32,256]{2,1,0:T(8,128)} collective-permute-done((f32[96,32,256]{2,1,0:T(8,128)}, f32[96,32,256]{2,1,0:T(8,128)}, u32[]{:S(2)}, u32[]{:S(2)}) %collective-permute-start.2) | collective-permute-done | bytes 3145760 | tf_op jit(solution)/shard_map/ppermute | solution.py:16
  80.7 3.9 collective-permute-done.3
  84.7 5.9 pad_maximum_fusion
  90.6 11.6 copy.69
  102.2 2.5 broadcast_in_dim.5
  104.7 38.0 %while.28 = (s32[]{:T(128)}, f32[32,96,256]{1,0,2:T(8,128)}, f32[256,65]{1,0:T(8,128)S(1)}, f32[96,96,256]{1,0,2:T(8,128)}, s32[96,32]{0,1:T(8,128)S(1)}, /*index=5*/s32[]{:T(128)}, s32[]{:T(128)}, s32[]{:T(128)}, s32[]{:T(128)}) while((s32[]{:T(128)}, f32[32,96,256]{1,0,2:T(8,128)}, f32[256,65]{1,0:T(8,128)S(1)}, ...), condition=%wide.region_1.0_spmd.clone, body=%wide.region_0.0_spmd.clone.sunk | while | flops 190322688 | bytes 2917519 | solution.py:62
  105.5 4.0 fusion.193
  110.2 4.0 fusion.193
  115.0 3.9 fusion.193
  119.7 3.9 fusion.193
  124.5 3.9 fusion.193
  129.2 3.9 fusion.193
  134.0 3.9 fusion.193
  138.7 3.9 fusion.193
  142.6 2.5 broadcast_in_dim.4
  145.1 31.1 %while.29 = (s32[]{:T(128)}, f32[32,32,256]{0,1,2:T(8,128)}, f32[256,65]{1,0:T(8,128)S(1)}, f32[32,96,256]{1,0,2:T(8,128)}, s32[96,32]{0,1:T(8,128)S(1)}, /*index=5*/s32[]{:T(128)}, s32[]{:T(128)}, s32[]{:T(128)}, s32[]{:T(128)}) while((s32[]{:T(128)}, f32[32,32,256]{0,1,2:T(8,128)}, f32[256,65]{1,0:T(8,128)S(1)}, ...), condition=%wide.region_3.0_spmd.clone, body=%wide.region_2.0_spmd.clone.sunk | while | flops 114825224 | bytes 1868943 | solution.py:62
  145.9 3.1 fusion.199
  149.8 3.1 fusion.199
  153.6 3.1 fusion.199
  157.5 3.1 fusion.199
  161.4 3.1 fusion.199
  165.3 3.1 fusion.199
  169.2 3.1 fusion.199
  173.1 3.1 fusion.199
  176.2 4.7 copy.71
  180.9 4.3 all-to-all-start
  185.9 3.9 multiply_reduce_fusion
  189.9 100.9 %psum.123 = f32[]{:T(128)} all-reduce(f32[]{:T(128)} %multiply_reduce_fusion), channel_id=1, replica_groups=mesh['sx'=8,'sy'=8,'af'=4] {'sx','sy','af'}, use_global_device_ids=true, to_apply=%region_11.14 | all-reduce | flops 1 | bytes 8 | tf_op jit(solution)/shard_map/psum | solution.py:73
  293.5 23.6 %psum.121 = f32[32,32]{0,1:T(8,128)S(1)} all-reduce(f32[32,32]{0,1:T(8,128)S(1)} %fusion.79), channel_id=1, replica_groups=mesh['sx'=8,'sy'=8,'af'=4] {'sx'}, use_global_device_ids=true, to_apply=%region_8.11 | all-reduce | flops 1024 | bytes 8192 | tf_op jit(solution)/shard_map/psum | solution.py:89
  317.1 134.7 %psum.122 = f32[32,32]{0,1:T(8,128)S(1)} all-reduce(f32[32,32]{0,1:T(8,128)S(1)} %psum.121), channel_id=1, replica_groups=mesh['sx'=8,'sy'=8,'af'=4] {'sy','af'}, use_global_device_ids=true, to_apply=%region_9.12 | all-reduce | flops 1024 | bytes 8192 | tf_op jit(solution)/shard_map/psum | solution.py:88
  451.9 2.9 cholesky.160
  458.9 65.5 %all-reduce.9.cloned.1.call-done = f32[1024,32]{0,1:T(8,128)} async-done(((f32[1024,32]{0,1:T(8,128)}), f32[1024,32]{0,1:T(8,128)}) %all-reduce.9.cloned.1.call-update) | async-done | bytes 131088 | tf_op jit(solution)/shard_map/psum | solution.py:89
  524.7 144.4 %all-reduce.11.cloned.1.call-done = f32[1024,32]{0,1:T(8,128)} async-done(((f32[1024,32]{0,1:T(8,128)}), f32[1024,32]{0,1:T(8,128)}) %all-reduce.11.cloned.1.call-update) | async-done | bytes 131088 | tf_op jit(solution)/shard_map/psum | solution.py:88
  673.9 2.9 cholesky.171
  684.0 23.5 %psum.126 = f32[32,32]{0,1:T(8,128)S(1)} all-reduce(f32[32,32]{0,1:T(8,128)S(1)} %fusion.85), channel_id=1, replica_groups=mesh['sx'=8,'sy'=8,'af'=4] {'sx'}, use_global_device_ids=true, to_apply=%region_16.19 | all-reduce | flops 1024 | bytes 8192 | tf_op jit(solution)/shard_map/psum | solution.py:89
  707.6 135.1 %psum.127 = f32[32,32]{0,1:T(8,128)S(1)} all-reduce(f32[32,32]{0,1:T(8,128)S(1)} %psum.126), channel_id=1, replica_groups=mesh['sx'=8,'sy'=8,'af'=4] {'sy','af'}, use_global_device_ids=true, to_apply=%region_17.20 | all-reduce | flops 1024 | bytes 8192 | tf_op jit(solution)/shard_map/psum | solution.py:88
  842.7 2.9 cholesky.182
  847.0 2.4 custom-call.16
  849.7 65.5 %all-reduce.13.cloned.1.call-done = f32[1024,32]{0,1:T(8,128)} async-done(((f32[1024,32]{0,1:T(8,128)}), f32[1024,32]{0,1:T(8,128)}) %all-reduce.13.cloned.1.call-update) | async-done | bytes 131088 | tf_op jit(solution)/shard_map/psum | solution.py:89
  915.5 144.3 %all-reduce.15.cloned.1.call-done = f32[1024,32]{0,1:T(8,128)} async-done(((f32[1024,32]{0,1:T(8,128)}), f32[1024,32]{0,1:T(8,128)}) %all-reduce.15.cloned.1.call-update) | async-done | bytes 131088 | tf_op jit(solution)/shard_map/psum | solution.py:88
  1064.6 2.9 cholesky.193
  1068.9 2.4 custom-call.17
  1074.7 23.5 %psum.130 = f32[32,32]{0,1:T(8,128)S(1)} all-reduce(f32[32,32]{0,1:T(8,128)S(1)} %fusion.91), channel_id=1, replica_groups=mesh['sx'=8,'sy'=8,'af'=4] {'sx'}, use_global_device_ids=true, to_apply=%region_22.25 | all-reduce | flops 1024 | bytes 8192 | tf_op jit(solution)/shard_map/psum | solution.py:89
  1098.3 135.1 %psum.131 = f32[32,32]{0,1:T(8,128)S(1)} all-reduce(f32[32,32]{0,1:T(8,128)S(1)} %psum.130), channel_id=1, replica_groups=mesh['sx'=8,'sy'=8,'af'=4] {'sy','af'}, use_global_device_ids=true, to_apply=%region_23.26 | all-reduce | flops 1024 | bytes 8192 | tf_op jit(solution)/shard_map/psum | solution.py:88
  1233.4 2.9 cholesky.204
  1237.7 2.4 custom-call.18
  1240.4 65.5 %all-reduce.17.cloned.1.call-done = f32[1024,32]{0,1:T(8,128)} async-done(((f32[1024,32]{0,1:T(8,128)}), f32[1024,32]{0,1:T(8,128)}) %all-reduce.17.cloned.1.call-update) | async-done | bytes 131088 | tf_op jit(solution)/shard_map/psum | solution.py:89
  1306.4 144.1 %all-reduce.19.cloned.1.call-done = f32[1024,32]{0,1:T(8,128)} async-done(((f32[1024,32]{0,1:T(8,128)}), f32[1024,32]{0,1:T(8,128)}) %all-reduce.19.cloned.1.call-update) | async-done | bytes 131088 | tf_op jit(solution)/shard_map/psum | solution.py:88
  1455.3 2.9 cholesky.215
  1459.5 2.4 custom-call.19
  1465.4 23.5 %psum.134 = f32[32,32]{0,1:T(8,128)S(1)} all-reduce(f32[32,32]{0,1:T(8,128)S(1)} %fusion.97), channel_id=1, replica_groups=mesh['sx'=8,'sy'=8,'af'=4] {'sx'}, use_global_device_ids=true, to_apply=%region_28.31 | all-reduce | flops 1024 | bytes 8192 | tf_op jit(solution)/shard_map/psum | solution.py:89
  1488.9 135.1 %psum.135 = f32[32,32]{0,1:T(8,128)S(1)} all-reduce(f32[32,32]{0,1:T(8,128)S(1)} %psum.134), channel_id=1, replica_groups=mesh['sx'=8,'sy'=8,'af'=4] {'sy','af'}, use_global_device_ids=true, to_apply=%region_29.32 | all-reduce | flops 1024 | bytes 8192 | tf_op jit(solution)/shard_map/psum | solution.py:88
  1624.1 2.9 cholesky.226
  1631.1 65.5 %all-reduce.21.cloned.1.call-done = f32[1024,32]{0,1:T(8,128)} async-done(((f32[1024,32]{0,1:T(8,128)}), f32[1024,32]{0,1:T(8,128)}) %all-reduce.21.cloned.1.call-update) | async-done | bytes 131088 | tf_op jit(solution)/shard_map/psum | solution.py:89
  1696.8 144.5 %all-reduce.23.cloned.1.call-done = f32[1024,32]{0,1:T(8,128)} async-done(((f32[1024,32]{0,1:T(8,128)}), f32[1024,32]{0,1:T(8,128)}) %all-reduce.23.cloned.1.call-update) | async-done | bytes 131088 | tf_op jit(solution)/shard_map/psum | solution.py:88
  1846.1 2.9 cholesky.237
  1856.7 4.2 all-to-all-start.1
  1861.5 10.3 all-to-all-done.1
  (159 shorter events, 79.0 us)
Async XLA Ops:
  7.9 18.7 copy-start
  7.9 18.8 %copy-start.1 = (f32[256,65]{0,1:T(8,128)S(1)}, f32[256,65]{0,1:T(8,128)}, u32[]{:S(2)}) copy-start(f32[256,65]{0,1:T(8,128)} %param.15) | copy-start | bytes 199684
  9.4 4.0 collective-permute-start
  11.2 5.9 collective-permute-start.1
  19.1 61.7 %collective-permute-start.2 = (f32[96,32,256]{2,1,0:T(8,128)}, f32[96,32,256]{2,1,0:T(8,128)}, u32[]{:S(2)}, u32[]{:S(2)}) collective-permute-start(f32[96,32,256]{2,1,0:T(8,128)} %pad_maximum_fusion.1), channel_id=1, source_target_pairs={{0,4},{4,8},{8,12},{12,16},{16,20},{20,24},{24,28},{1,5},{5,9},{9,... | collective-permute-start | bytes 9437192 | tf_op jit(solution)/shard_map/ppermute | solution.py:16
  22.9 61.8 %collective-permute-start.3 = (f32[96,32,256]{2,1,0:T(8,128)}, f32[96,32,256]{2,1,0:T(8,128)}, u32[]{:S(2)}, u32[]{:S(2)}) collective-permute-start(f32[96,32,256]{2,1,0:T(8,128)} %pad_maximum_fusion.1), channel_id=1, source_target_pairs={{4,0},{8,4},{12,8},{16,12},{20,16},{24,20},{28,24},{5,1},{9,5},{13... | collective-permute-start | bytes 9437192 | tf_op jit(solution)/shard_map/ppermute | solution.py:19
  176.2 9.0 copy-start.2
  180.9 109.9 %all-to-all-start = ((f32[4,256,256]{2,1,0:T(8,128)}), f32[4,256,256]{2,1,0:T(8,128)S(1)}, u32[]{:S(2)}, u32[]{:S(2)}) async-start(f32[4,256,256]{2,1,0:T(8,128)} %bitcast), calls=%async_computation | async-start | bytes 2097152 | tf_op jit(solution)/shard_map/all_to_all | solution.py:80
  185.2 339.2 %all-reduce.9.cloned.1.call-start = ((), (), s32[]{:S(2)}) async-start(), calls=%async_computation.2 | async-start | bytes 262144 | tf_op jit(solution)/shard_map/psum | solution.py:89
  458.6 210.5 %all-reduce.11.cloned.1.call-start = ((), (), s32[]{:S(2)}) async-start(), calls=%async_computation.3 | async-start | bytes 262144 | tf_op jit(solution)/shard_map/psum | solution.py:88
  524.4 390.8 %all-reduce.13.cloned.1.call-start = ((), (), s32[]{:S(2)}) async-start(), calls=%async_computation.4 | async-start | bytes 262144 | tf_op jit(solution)/shard_map/psum | solution.py:89
  849.5 210.3 %all-reduce.15.cloned.1.call-start = ((), (), s32[]{:S(2)}) async-start(), calls=%async_computation.5 | async-start | bytes 262144 | tf_op jit(solution)/shard_map/psum | solution.py:88
  915.3 390.7 %all-reduce.17.cloned.1.call-start = ((), (), s32[]{:S(2)}) async-start(), calls=%async_computation.6 | async-start | bytes 262144 | tf_op jit(solution)/shard_map/psum | solution.py:89
  1240.2 210.3 %all-reduce.19.cloned.1.call-start = ((), (), s32[]{:S(2)}) async-start(), calls=%async_computation.7 | async-start | bytes 262144 | tf_op jit(solution)/shard_map/psum | solution.py:88
  1305.9 390.7 %all-reduce.21.cloned.1.call-start = ((), (), s32[]{:S(2)}) async-start(), calls=%async_computation.8 | async-start | bytes 262144 | tf_op jit(solution)/shard_map/psum | solution.py:89
  1630.8 210.5 %all-reduce.23.cloned.1.call-start = ((), (), s32[]{:S(2)}) async-start(), calls=%async_computation.9 | async-start | bytes 262144 | tf_op jit(solution)/shard_map/psum | solution.py:88
  1856.7 15.1 all-to-all-start.1
Sparse Core Ops, SparseCore 0:
  458.8 65.5 all-reduce.8
  527.9 141.2 all-reduce.10
  849.6 65.5 all-reduce.12
  918.5 141.2 all-reduce.14
  1240.3 65.5 all-reduce.16
  1309.2 141.2 all-reduce.18
  1631.0 65.5 all-reduce.20
  1700.0 141.2 all-reduce.22
